TPU v7x, 32 devices: a whole 2x2x4 slice. The times are simulated.
32 devices in a mesh: role: 2 (over x), grp: 8 (over z, y), tp: 2 (over core).
Axes of the slice: x: 2, y: 2, z: 4, core: 2. Of those that a mesh axis runs over, the one named last changes fastest.
Arguments:
- q_new: bfloat16 [256, 4096], P('grp', ('role', 'tp')), may hold values from -9 to 9
- k_new: bfloat16 [256, 512], P('grp', ('role', 'tp')), may hold values from -6 to 6
- v_new: bfloat16 [256, 512], P('grp', ('role', 'tp')), may hold values from -6 to 6
- k_cache: bfloat16 [256, 128, 512], P('grp', None, ('role', 'tp')), may hold values from -9 to 9
- v_cache: bfloat16 [256, 128, 512], P('grp', None, ('role', 'tp')), may hold values from -6 to 6
- cache_len: int32 [256], P('grp'), may hold values from 1 to 127
- cycle_start: int32 [256], P('grp'), may hold values from 0 to 127
- residual: bfloat16 [256, 2880], P('grp', ('role', 'tp')), may hold values from -6 to 6
- out_proj: bfloat16 [4096, 2880], P(('role', 'tp')), may hold values from -0.09375 to 0.09375
- norm_gain: float32 [2880], replicated, may hold values from 0.25 to 1.75
- router: bfloat16 [2880, 8], P(('role', 'tp')), may hold values from -0.21875 to 0.21875
- route_ids: int32 [256, 4], P('grp'), may hold values from 0 to 7, all different within a row; in each aligned block of 32 rows (0 to 31, 32 to 63, ...) at most 18 rows name the same one
- w_gate: bfloat16 [8, 2880, 1440], P('grp', None, ('role', 'tp')), may hold values from -0.109375 to 0.109375
- w_up: bfloat16 [8, 2880, 1440], P('grp', None, ('role', 'tp')), may hold values from -0.109375 to 0.109375
- w_down: bfloat16 [8, 1440, 2880], P('grp', ('role', 'tp')), may hold values from -0.15625 to 0.15625
Outputs:
- attended: bfloat16 [256, 2880], P('grp', ('role', 'tp'))
- expert_mix: bfloat16 [256, 2880], P('grp', ('role', 'tp'))
Inputs may be any that keep to these rules, and one draw needn't show every extreme that they name: `route_ids`: the 4 experts of a token differ. Among the tokens of one grp index (aligned blocks of 32 tokens) no expert is named more than 18 times, a bound that some block reaches.
All inputs are finite; a program needn't handle non-finite values.
Results may differ from a plain program's by a relative error of at most 0.017.
Values may be sent and summed in bfloat16 or wider, within the bound.
No kernel may reach another device: no remote copies, remote signals or barrier semaphores. Data moves between devices by JAX's collectives and lax.ppermute only.
A program may use at most 64 MiB of HBM per device.

v0:
```python
import jax
import jax.numpy as jnp
from jax import lax
from jax.sharding import PartitionSpec as P

HEADS = 64
KV_HEADS = 8
HD = 64
epsilon = 1e-05


def attend(q_new, k_new, v_new, k_cache, v_cache, cache_len, cycle_start):
    tokens = q_new.shape[0]
    window = k_cache.shape[1]
    kv_local = k_new.shape[1] // HD
    grouped = HEADS // KV_HEADS
    queries = q_new.reshape(tokens, kv_local, grouped, HD)
    cached_keys = k_cache.reshape(tokens, window, kv_local, HD)
    cached_values = v_cache.reshape(tokens, window, kv_local, HD)
    own_key = k_new.reshape(tokens, kv_local, HD)
    own_value = v_new.reshape(tokens, kv_local, HD)
    factor = HD ** (-0.5)
    scores = (
        jnp.einsum("tkgd,tskd->tkgs", queries, cached_keys, preferred_element_type=jnp.float32)
        * factor
    )
    own_score = (
        jnp.einsum("tkgd,tkd->tkg", queries, own_key, preferred_element_type=jnp.float32) * factor
    )
    positions = jnp.arange(window, dtype=jnp.int32)
    usable = (positions[None, :] - cycle_start[:, None]) % window < cache_len[:, None]
    usable = usable[:, None, None, :]
    masked = jnp.where(usable, scores, -1e30)
    highest = jnp.maximum(jnp.max(masked, axis=3), own_score)
    lifted = jnp.where(usable, jnp.exp(masked - highest[..., None]), 0.0)
    own_lift = jnp.exp(own_score - highest)
    denominator = jnp.sum(lifted, axis=3) + own_lift
    weights = (lifted / denominator[..., None]).astype(jnp.bfloat16)
    own_weight = (own_lift / denominator).astype(jnp.bfloat16)
    combined = jnp.einsum(
        "tkgs,tskd->tkgd", weights, cached_values, preferred_element_type=jnp.float32
    )
    combined = (
        combined
        + own_weight.astype(jnp.float32)[..., None] * own_value.astype(jnp.float32)[:, :, None, :]
    )
    return combined.reshape(tokens, -1).astype(jnp.bfloat16)


def slot_tables(route_ids, logits, capacity):
    experts_count = logits.shape[1]
    named = route_ids[:, :, None] == jnp.arange(experts_count, dtype=jnp.int32)
    chosen = jnp.sum(jnp.where(named, logits[:, None, :], 0.0), axis=2)
    lifted = jnp.exp(chosen)
    route_weight = lifted / jnp.sum(lifted, axis=1, keepdims=True)
    counts = jnp.sum(named.astype(jnp.int32), axis=1)
    earlier = jnp.cumsum(counts, axis=0) - counts
    ranks = jnp.sum(jnp.where(named, earlier[:, None, :], 0), axis=2)
    placed = named[:, :, :, None] & (
        ranks[:, :, None, None] == jnp.arange(capacity, dtype=jnp.int32)
    )
    select = jnp.sum(placed.astype(jnp.float32), axis=1).reshape(route_ids.shape[0], -1)
    mixing = jnp.sum(jnp.where(placed, route_weight[:, :, None, None], 0.0), axis=1).reshape(
        route_ids.shape[0], -1
    )
    return (select, mixing)


def serve(received, w_gate, w_up, w_down):
    sources = received.shape[0]
    items = received.shape[1]
    inputs = received.reshape(sources * items, received.shape[2])
    gate_lin = jnp.dot(inputs, w_gate[0], preferred_element_type=jnp.float32)
    up_lin = jnp.dot(inputs, w_up[0], preferred_element_type=jnp.float32)
    activated = (gate_lin * jax.nn.sigmoid(1.702 * gate_lin) * (up_lin + 1.0)).astype(jnp.bfloat16)
    partial_out = jnp.dot(activated, w_down[0], preferred_element_type=jnp.float32).reshape(
        sources, items, -1
    )
    rounded = lax.optimization_barrier(partial_out.astype(jnp.bfloat16))
    return lax.all_to_all(rounded, "grp", split_axis=0, concat_axis=0, tiled=True)


def local(
    q_new,
    k_new,
    v_new,
    k_cache,
    v_cache,
    cache_len,
    cycle_start,
    residual,
    out_proj,
    norm_gain,
    router,
    route_ids,
    w_gate,
    w_up,
    w_down,
):
    share = lax.axis_index(("role", "tp"))
    quarter = residual.shape[1]
    heads_out = attend(q_new, k_new, v_new, k_cache, v_cache, cache_len, cycle_start)
    projected = jnp.dot(heads_out, out_proj, preferred_element_type=jnp.float32)
    stream = lax.all_gather(residual, ("role", "tp"), axis=1, tiled=True).astype(
        jnp.float32
    ) + lax.psum(projected.astype(jnp.bfloat16), ("role", "tp")).astype(jnp.float32)
    scale = lax.rsqrt(jnp.mean(stream * stream, axis=1, keepdims=True) + epsilon)
    outgoing = (stream * scale * norm_gain).astype(jnp.bfloat16)
    own_normed = lax.dynamic_slice_in_dim(outgoing, share * quarter, quarter, 1)
    attended = lax.dynamic_slice_in_dim(stream, share * quarter, quarter, 1)
    logits = lax.psum(
        jnp.dot(own_normed, router, preferred_element_type=jnp.float32), ("role", "tp")
    )
    tokens = route_ids.shape[0]
    experts_count = logits.shape[1]
    capacity = max(3, tokens * route_ids.shape[1] // experts_count + 2)
    select, mixing = slot_tables(route_ids, logits, capacity)
    outbound = jnp.einsum(
        "ts,tf->sf", select.astype(jnp.bfloat16), outgoing, preferred_element_type=jnp.float32
    )
    outbound = outbound.astype(jnp.bfloat16).reshape(experts_count, capacity, -1)
    returned = serve(
        lax.all_to_all(outbound, "grp", split_axis=0, concat_axis=0, tiled=True),
        w_gate,
        w_up,
        w_down,
    )
    stacked = returned.reshape(-1, returned.shape[2]).astype(jnp.float32)
    combined = jnp.dot(mixing, stacked, precision=lax.Precision.HIGHEST)
    combined = lax.psum_scatter(
        combined.astype(jnp.bfloat16), ("role", "tp"), scatter_dimension=1, tiled=True
    ).astype(jnp.float32)
    return (attended.astype(jnp.bfloat16), combined.astype(jnp.bfloat16))


def solution(mesh):
    placed = (
        P("grp", ("role", "tp")),
        P("grp", ("role", "tp")),
        P("grp", ("role", "tp")),
        P("grp", None, ("role", "tp")),
        P("grp", None, ("role", "tp")),
        P("grp"),
        P("grp"),
        P("grp", ("role", "tp")),
        P(("role", "tp"), None),
        P(),
        P(("role", "tp"), None),
        P("grp", None),
        P("grp", None, ("role", "tp")),
        P("grp", None, ("role", "tp")),
        P("grp", ("role", "tp"), None),
    )
    return jax.shard_map(
        local,
        mesh=mesh,
        in_specs=placed,
        out_specs=(P("grp", ("role", "tp")), P("grp", ("role", "tp"))),
        check_vma=False,
    )
```

profile of v0, /device:TPU:0, one launch (start us, length us, event | category | flops | bytes accessed | tf_op | source)
XLA Modules:
  0.0 172.5 jit_solution(14774596593833444122)
XLA Ops:
  7.2 0.9 reshape.146
  8.2 0.8 reshape.137
  8.9 1.0 reshape.131
  10.2 0.4 copy-done.2
  10.7 1.6 copy.52
  12.4 1.4 fusion.37
  14.0 0.3 fusion.19
  14.4 0.7 copy.58
  15.1 1.6 copy.57
  16.8 2.1 %fusion.13 = bf16[32,2,8,64]{3,2,1,0:T(8,128)(2,1)} fusion(bf16[32,128,2,64]{1,3,2,0:T(8,128)(2,1)S(1)} %bitcast.66, f32[32,2,8,128]{3,2,1,0:T(8,128)S(1)} %get-tuple-element.9, f32[32,2,64]{2,1,0:T(2,128)S(1)} %reshape.137, f32[32,2,8]{2,1,0:T(2,128)} %copy.58, f32[32,2,8]{2,1,0:T(2,128)S(1)} %copy.56, f32[32,2,8]{2,1,0:T(2,128)S(1)} %copy.54, ...), kind=kOutput, calls=%fused_computation.15 | convolution fusion | flops 8749056 | bytes 1402880 | tf_op jit(solution)/shard_map/tkgs,tskd->tkgd/dot_general | solution.py:40
  18.9 1.0 convert_element_type.74
  20.0 5.2 %convolution_convert_fusion.2 = bf16[32,2880]{1,0:T(8,128)(2,1)} fusion(bf16[32,1024]{1,0:T(8,128)(2,1)S(1)} %convert_element_type.74, bf16[1024,2880]{0,1:T(8,128)(2,1)} %param.23), kind=kOutput, calls=%fused_computation.4 | convolution fusion | flops 188835840 | bytes 6148096 | tf_op jit(solution)/shard_map/dot_general | solution.py:103
  25.6 6.9 %all-gather = bf16[4,720,32]{1,2,0:T(8,128)(2,1)S(1)} all-gather(bf16[1,720,32]{1,2,0:T(8,128)(2,1)S(1)} %bitcast.68), channel_id=1, replica_groups=mesh['role'=2,'grp'=8,'tp'=2] {'role','tp'}, dimensions={0}, use_global_device_ids=true | all-gather | bytes 230400 | tf_op jit(solution)/shard_map/all_gather | solution.py:104
  32.6 0.2 reshape.140
  32.9 27.2 %all-reduce.2.cloned.1.call-done = bf16[32,2880]{1,0:T(8,128)(2,1)} async-done(((bf16[32,2880]{1,0:T(8,128)(2,1)}), bf16[32,2880]{1,0:T(8,128)(2,1)}) %all-reduce.2.cloned.1.call-update) | async-done | bytes 184336 | tf_op jit(solution)/shard_map/psum | solution.py:106
  60.0 1.1 multiply_reduce_fusion
  61.1 0.7 copy-done.1
  62.0 0.2 fusion.25
  62.2 5.7 %psum.15 = f32[32,8]{0,1:T(8,128)S(1)} all-reduce(f32[32,8]{0,1:T(8,128)S(1)} %fusion.25), channel_id=1, replica_groups=mesh['role'=2,'grp'=8,'tp'=2] {'role','tp'}, use_global_device_ids=true, to_apply=%region_7.8 | all-reduce | flops 256 | bytes 2048 | tf_op jit(solution)/shard_map/psum | solution.py:111
  68.4 1.3 convolution_convert_fusion.1
  69.7 1.4 reshape.135
  71.1 33.4 %all_to_all.10 = bf16[8,18,2880]{2,1,0:T(8,128)(2,1)} all-to-all(bf16[8,18,2880]{2,1,0:T(8,128)(2,1)S(1)} %reshape.135), channel_id=1, replica_groups=mesh['role'=2,'grp'=8,'tp'=2] {'grp'}, dimensions={0} | all-to-all | bytes 1658880 | tf_op jit(solution)/shard_map/all_to_all | solution.py:123
  104.6 1.7 reshape.136
  106.3 2.6 %fusion.4 = f32[144,360]{1,0:T(8,128)S(1)} fusion(bf16[144,2880]{1,0:T(8,128)(2,1)S(1)} %reshape.136, bf16[1,2880,360]{1,2,0:T(8,128)(2,1)} %param.27), kind=kOutput, calls=%fused_computation.8 | convolution fusion | flops 298598400 | bytes 3110400 | tf_op jit(solution)/shard_map/dot_general | solution.py:73
  108.9 0.8 fusion.14
  109.8 0.8 convolution_convert_fusion
  110.6 30.5 %all_to_all.11 = bf16[8,18,2880]{2,1,0:T(8,128)(2,1)S(1)} all-to-all(bf16[8,18,2880]{2,1,0:T(8,128)(2,1)S(1)} %convolution_convert_fusion), channel_id=1, replica_groups=mesh['role'=2,'grp'=8,'tp'=2] {'grp'}, dimensions={0} | all-to-all | bytes 1658880 | tf_op jit(solution)/shard_map/all_to_all | solution.py:80
  141.1 0.8 fusion
  141.9 1.2 copy.66
  143.1 1.6 dynamic-slice_convert_fusion
  144.7 19.3 %reduce-scatter.4.cloned.1.call-done = bf16[720,32]{1,0:T(8,128)(2,1)} async-done(((bf16[2880,32]{1,0:T(8,128)(2,1)}), bf16[720,32]{1,0:T(8,128)(2,1)}) %reduce-scatter.4.cloned.1.call-update) | async-done | bytes 46096
  164.0 1.7 copy.67
  (49 shorter events, 1.8 us)
Async XLA Ops:
  7.2 102.6 %copy-start = (bf16[1,360,2880]{2,1,0:T(8,128)(2,1)S(1)}, bf16[1,360,2880]{2,1,0:T(8,128)(2,1)}, u32[]{:S(2)}) copy-start(bf16[1,360,2880]{2,1,0:T(8,128)(2,1)} %param.29) | copy-start | bytes 6220804
  7.2 5.1 %copy-start.8 = (s32[32]{0:T(128)S(1)}, s32[32]{0:T(128)}, u32[]{:S(2)}) copy-start(s32[32]{0:T(128)} %param.21) | copy-start | bytes 388
  7.2 5.1 %copy-start.7 = (s32[32]{0:T(128)S(1)}, s32[32]{0:T(128)}, u32[]{:S(2)}) copy-start(s32[32]{0:T(128)} %param.20) | copy-start | bytes 388
  7.2 52.8 %all-reduce.2.cloned.1.call-start = ((), (), s32[]{:S(2)}) async-start(), calls=%async_computation.3 | async-start | bytes 376832 | tf_op jit(solution)/shard_map/psum | solution.py:106
  10.0 0.6 copy-start.2
  19.9 5.3 %copy-start.4 = (s32[32,4]{0,1:T(4,128)S(1)}, s32[32,4]{0,1:T(4,128)}, u32[]{:S(2)}) copy-start(s32[32,4]{0,1:T(4,128)} %param.26) | copy-start | bytes 1540
  20.0 5.6 %copy-start.3 = (bf16[32,720]{1,0:T(8,128)(2,1)S(1)}, bf16[32,720]{1,0:T(8,128)(2,1)}, u32[]{:S(2)}) copy-start(bf16[32,720]{1,0:T(8,128)(2,1)} %param.22) | copy-start | bytes 138244
  25.2 36.7 %copy-start.6 = (f32[2880]{0:T(1024)S(1)}, f32[2880]{0:T(1024)}, u32[]{:S(2)}) copy-start(f32[2880]{0:T(1024)} %param.24) | copy-start | bytes 34564
  25.2 36.8 %copy-start.5 = (bf16[720,8]{0,1:T(8,128)(2,1)S(1)}, bf16[720,8]{0,1:T(8,128)(2,1)}, u32[]{:S(2)}) copy-start(bf16[720,8]{0,1:T(8,128)(2,1)} %param.25) | copy-start | bytes 34564
  25.2 138.8 %reduce-scatter.4.cloned.1.call-start = ((), (), s32[]{:S(2)}) async-start(), calls=%async_computation.4 | async-start | bytes 921600
  61.1 0.8 copy-start.1
  106.3 2.6 %copy-start.9 = (bf16[1,2880,360]{1,2,0:T(8,128)(2,1)S(1)}, bf16[1,2880,360]{1,2,0:T(8,128)(2,1)}, u32[]{:S(2)}) copy-start(bf16[1,2880,360]{1,2,0:T(8,128)(2,1)} %param.28) | copy-start | bytes 6220804
Sparse Core Ops, SparseCore 0:
  25.3 34.6 all-reduce.1
  143.2 20.7 reduce-scatter.3
where the time goes:
time: 173 us
  blocking collectives  76.6 us (44%)
  waiting for transfers between devices  46.5 us (27%)
  local copies, waits for them, and re-layouts  17.7 us (10%)
  matrix products  15.4 us (9%)
  between operations  14.3 us (8%)
  other arithmetic  1.84 us (1%)
    all_to_all x1, blocking collectives, local(): lax.all_to_all(outbound, 'grp', split_axis=0, concat_axis=0, tiled=True)  33.4 us
    all_to_all x1, blocking collectives, serve(): lax.all_to_all(rounded, 'grp', split_axis=0, concat_axis=0, tiled=True)  30.5 us
    psum x1, waiting for transfers between devices, local(): lax.psum(projected.astype(jnp.bfloat16), ('role', 'tp')).astype(jnp.float32)  27.2 us
    unnamed x3, waiting for transfers between devices  19.3 us
    unnamed x24, local copies, waits for them, and re-layouts  7.26 us
    all_gather x1, blocking collectives, local(): lax.all_gather(residual, ('role', 'tp'), axis=1, tiled=True)  6.87 us
    psum x1, blocking collectives, local(): lax.psum(jnp.dot(own_normed, router, preferred_element_type=jnp.float32),...  5.74 us
    dot_general x1, matrix products, local(): projected = jnp.dot(heads_out, out_proj, preferred_element_type=jnp.float32)  5.22 us
  transfers between devices with their start and end apart: 2, of which 2 were waited for; matrix products, arithmetic and copies ran while one was open for 1% of the time, Pallas kernels for 0%

commit v1 on v0

--- a/solution.py
+++ b/solution.py
@@ -2,6 +2,7 @@
 import jax.numpy as jnp
 from jax import lax
 from jax.sharding import PartitionSpec as P
+from jax.lax import psum
 
 HEADS = 64
 KV_HEADS = 8
@@ -103,7 +104,7 @@
     projected = jnp.dot(heads_out, out_proj, preferred_element_type=jnp.float32)
     stream = lax.all_gather(residual, ("role", "tp"), axis=1, tiled=True).astype(
         jnp.float32
-    ) + lax.psum(projected.astype(jnp.bfloat16), ("role", "tp")).astype(jnp.float32)
+    ) + psum(psum(projected.astype(jnp.bfloat16), "tp"), "role").astype(jnp.float32)
     scale = lax.rsqrt(jnp.mean(stream * stream, axis=1, keepdims=True) + epsilon)
     outgoing = (stream * scale * norm_gain).astype(jnp.bfloat16)
     own_normed = lax.dynamic_slice_in_dim(outgoing, share * quarter, quarter, 1)

time: 173 us -> 185 us (1.069)
  waiting for transfers between devices: 46.5 us -> 58.1 us
    psum x1 -> x2, waiting for transfers between devices: 27.2 us -> 39.1 us  [the longest x1 25.8 us: local(): psum(psum(projected.astype(jnp.bfloat16), 'tp'), 'role').astype(jnp.float32)]
    unnamed x3 -> x4, waiting for transfers between devices: 19.3 us -> 19 us
  transfers between devices with their start and end apart: 2 -> 3, of which waited for: 2 -> 3; matrix products, arithmetic and copies ran while one was open for 1% -> 1% of each run, Pallas kernels for 0% -> 0%
where the time goes in v1:
time: 185 us; the launch traced here: 184 us
  blocking collectives  76.9 us (42%)
  waiting for transfers between devices  58.1 us (31%)
  local copies, waits for them, and re-layouts  17.7 us (10%)
  matrix products  15.5 us (8%)
  between operations  14 us (8%)
    all_to_all x1, blocking collectives, local(): lax.all_to_all(outbound, 'grp', split_axis=0, concat_axis=0, tiled=True)  33.4 us
    all_to_all x1, blocking collectives, serve(): lax.all_to_all(rounded, 'grp', split_axis=0, concat_axis=0, tiled=True)  30.8 us
    psum x1, waiting for transfers between devices, local(): psum(psum(projected.astype(jnp.bfloat16), 'tp'), 'role').astype(jnp.float32)  25.8 us
    unnamed x4, waiting for transfers between devices  19 us
    psum x1, waiting for transfers between devices, local(): psum(projected.astype(jnp.bfloat16), 'tp')  13.3 us
    unnamed x24, local copies, waits for them, and re-layouts  7.26 us
    all_gather x1, blocking collectives, local(): lax.all_gather(residual, ('role', 'tp'), axis=1, tiled=True)  6.87 us
    psum x1, blocking collectives, local(): lax.psum(jnp.dot(own_normed, router, preferred_element_type=jnp.float32),...  5.74 us
  transfers between devices with their start and end apart: 3, of which 3 were waited for; matrix products, arithmetic and copies ran while one was open for 1% of the time, Pallas kernels for 0%

profile of v1, /device:TPU:0, one launch (start us, length us, event | category | flops | bytes accessed | tf_op | source)
XLA Modules:
  0.0 184.1 jit_solution(5130874727245528129)
XLA Ops:
  7.2 0.9 reshape.146
  8.2 0.8 reshape.137
  8.9 1.0 reshape.131
  10.2 0.4 copy-done.2
  10.7 1.6 copy.52
  12.4 1.4 fusion.37
  14.0 0.3 fusion.19
  14.4 0.7 copy.58
  15.1 1.6 copy.57
  16.8 2.1 %fusion.13 = bf16[32,2,8,64]{3,2,1,0:T(8,128)(2,1)} fusion(bf16[32,128,2,64]{1,3,2,0:T(8,128)(2,1)S(1)} %bitcast.66, f32[32,2,8,128]{3,2,1,0:T(8,128)S(1)} %get-tuple-element.9, f32[32,2,64]{2,1,0:T(2,128)S(1)} %reshape.137, f32[32,2,8]{2,1,0:T(2,128)} %copy.58, f32[32,2,8]{2,1,0:T(2,128)S(1)} %copy.56, f32[32,2,8]{2,1,0:T(2,128)S(1)} %copy.54, ...), kind=kOutput, calls=%fused_computation.15 | convolution fusion | flops 8749056 | bytes 1402880 | tf_op jit(solution)/shard_map/tkgs,tskd->tkgd/dot_general | solution.py:41
  18.9 1.0 convert_element_type.74
  20.0 5.2 %convolution_convert_fusion.2 = bf16[32,2880]{1,0:T(8,128)(2,1)} fusion(bf16[32,1024]{1,0:T(8,128)(2,1)S(1)} %convert_element_type.74, bf16[1024,2880]{0,1:T(8,128)(2,1)} %param.23), kind=kOutput, calls=%fused_computation.4 | convolution fusion | flops 188835840 | bytes 6148096 | tf_op jit(solution)/shard_map/dot_general | solution.py:104
  25.5 6.9 %all-gather = bf16[4,720,32]{1,2,0:T(8,128)(2,1)S(1)} all-gather(bf16[1,720,32]{1,2,0:T(8,128)(2,1)S(1)} %bitcast.68), channel_id=1, replica_groups=mesh['role'=2,'grp'=8,'tp'=2] {'role','tp'}, dimensions={0}, use_global_device_ids=true | all-gather | bytes 230400 | tf_op jit(solution)/shard_map/all_gather | solution.py:105
  32.6 0.2 reshape.140
  32.8 13.3 %all-reduce.3.cloned.1.call-done = bf16[32,2880]{1,0:T(8,128)(2,1)} async-done(((bf16[32,2880]{1,0:T(8,128)(2,1)}), bf16[32,2880]{1,0:T(8,128)(2,1)}) %all-reduce.3.cloned.1.call-update) | async-done | bytes 184336 | tf_op jit(solution)/shard_map/psum | solution.py:107
  46.2 25.8 %all-reduce.5.cloned.1.call-done = bf16[32,2880]{1,0:T(8,128)(2,1)} async-done(((bf16[32,2880]{1,0:T(8,128)(2,1)}), bf16[32,2880]{1,0:T(8,128)(2,1)}) %all-reduce.5.cloned.1.call-update) | async-done | bytes 184336 | tf_op jit(solution)/shard_map/psum | solution.py:107
  72.0 1.1 multiply_reduce_fusion
  73.1 0.7 copy-done.1
  74.2 5.7 %psum.23 = f32[32,8]{0,1:T(8,128)S(1)} all-reduce(f32[32,8]{0,1:T(8,128)S(1)} %fusion.25), channel_id=1, replica_groups=mesh['role'=2,'grp'=8,'tp'=2] {'role','tp'}, use_global_device_ids=true, to_apply=%region_8.9 | all-reduce | flops 256 | bytes 2048 | tf_op jit(solution)/shard_map/psum | solution.py:112
  80.3 1.3 convolution_convert_fusion.1
  81.6 1.4 reshape.135
  83.1 33.4 %all_to_all.10 = bf16[8,18,2880]{2,1,0:T(8,128)(2,1)} all-to-all(bf16[8,18,2880]{2,1,0:T(8,128)(2,1)S(1)} %reshape.135), channel_id=1, replica_groups=mesh['role'=2,'grp'=8,'tp'=2] {'grp'}, dimensions={0} | all-to-all | bytes 1658880 | tf_op jit(solution)/shard_map/all_to_all | solution.py:124
  116.5 1.7 reshape.136
  118.3 2.6 %fusion.4 = f32[144,360]{1,0:T(8,128)S(1)} fusion(bf16[144,2880]{1,0:T(8,128)(2,1)S(1)} %reshape.136, bf16[1,2880,360]{1,2,0:T(8,128)(2,1)} %param.27), kind=kOutput, calls=%fused_computation.8 | convolution fusion | flops 298598400 | bytes 3110400 | tf_op jit(solution)/shard_map/dot_general | solution.py:74
  120.8 0.8 fusion.14
  121.7 0.8 convolution_convert_fusion
  122.5 30.8 %all_to_all.11 = bf16[8,18,2880]{2,1,0:T(8,128)(2,1)S(1)} all-to-all(bf16[8,18,2880]{2,1,0:T(8,128)(2,1)S(1)} %convolution_convert_fusion), channel_id=1, replica_groups=mesh['role'=2,'grp'=8,'tp'=2] {'grp'}, dimensions={0} | all-to-all | bytes 1658880 | tf_op jit(solution)/shard_map/all_to_all | solution.py:81
  153.3 0.8 fusion
  154.1 1.2 copy.66
  155.3 1.6 dynamic-slice_convert_fusion
  156.9 19.0 %reduce-scatter.4.cloned.1.call-done = bf16[720,32]{1,0:T(8,128)(2,1)} async-done(((bf16[2880,32]{1,0:T(8,128)(2,1)}), bf16[720,32]{1,0:T(8,128)(2,1)}) %reduce-scatter.4.cloned.1.call-update) | async-done | bytes 46096
  175.9 1.7 copy.67
  (52 shorter events, 2.1 us)
Async XLA Ops:
  7.2 114.6 %copy-start = (bf16[1,360,2880]{2,1,0:T(8,128)(2,1)S(1)}, bf16[1,360,2880]{2,1,0:T(8,128)(2,1)}, u32[]{:S(2)}) copy-start(bf16[1,360,2880]{2,1,0:T(8,128)(2,1)} %param.29) | copy-start | bytes 6220804
  7.2 5.1 %copy-start.8 = (s32[32]{0:T(128)S(1)}, s32[32]{0:T(128)}, u32[]{:S(2)}) copy-start(s32[32]{0:T(128)} %param.21) | copy-start | bytes 388
  7.2 5.1 %copy-start.7 = (s32[32]{0:T(128)S(1)}, s32[32]{0:T(128)}, u32[]{:S(2)}) copy-start(s32[32]{0:T(128)} %param.20) | copy-start | bytes 388
  7.2 38.9 %all-reduce.3.cloned.1.call-start = ((), (), s32[]{:S(2)}) async-start(), calls=%async_computation.3 | async-start | bytes 376832 | tf_op jit(solution)/shard_map/psum | solution.py:107
  10.0 0.6 copy-start.2
  19.9 5.3 %copy-start.4 = (s32[32,4]{0,1:T(4,128)S(1)}, s32[32,4]{0,1:T(4,128)}, u32[]{:S(2)}) copy-start(s32[32,4]{0,1:T(4,128)} %param.26) | copy-start | bytes 1540
  20.0 5.6 %copy-start.3 = (bf16[32,720]{1,0:T(8,128)(2,1)S(1)}, bf16[32,720]{1,0:T(8,128)(2,1)}, u32[]{:S(2)}) copy-start(bf16[32,720]{1,0:T(8,128)(2,1)} %param.22) | copy-start | bytes 138244
  25.2 48.6 %copy-start.6 = (f32[2880]{0:T(1024)S(1)}, f32[2880]{0:T(1024)}, u32[]{:S(2)}) copy-start(f32[2880]{0:T(1024)} %param.24) | copy-start | bytes 34564
  25.2 48.8 %copy-start.5 = (bf16[720,8]{0,1:T(8,128)(2,1)S(1)}, bf16[720,8]{0,1:T(8,128)(2,1)}, u32[]{:S(2)}) copy-start(bf16[720,8]{0,1:T(8,128)(2,1)} %param.25) | copy-start | bytes 34564
  25.2 46.8 %all-reduce.5.cloned.1.call-start = ((), (), s32[]{:S(2)}) async-start(), calls=%async_computation.4 | async-start | bytes 376832 | tf_op jit(solution)/shard_map/psum | solution.py:107
  46.2 129.8 %reduce-scatter.4.cloned.1.call-start = ((), (), s32[]{:S(2)}) async-start(), calls=%async_computation.5 | async-start | bytes 921600
  73.1 0.8 copy-start.1
  118.2 2.6 %copy-start.9 = (bf16[1,2880,360]{1,2,0:T(8,128)(2,1)S(1)}, bf16[1,2880,360]{1,2,0:T(8,128)(2,1)}, u32[]{:S(2)}) copy-start(bf16[1,2880,360]{1,2,0:T(8,128)(2,1)} %param.28) | copy-start | bytes 6220804
Sparse Core Ops, SparseCore 0:
  25.3 20.7 all-reduce.2
  48.4 23.5 all-reduce.4
  155.4 20.4 reduce-scatter.3
